TPU v7x, 32 devices: a whole 2x2x4 slice. The times are simulated.
32 devices in a mesh: dp: 4 (over z), neg: 8 (over y, x, core).
Axes of the slice: x: 2, y: 2, z: 4, core: 2. Of those that a mesh axis runs over, the one named last changes fastest.
Arguments:
- query_emb: bfloat16 [128, 32, 128], P(('dp', 'neg')), may hold values from -6 to 6
- positive: int32 [128], P(('dp', 'neg')), may hold values from 0 to 31
- passage_emb: bfloat16 [32, 512, 128], P(('dp', 'neg')), may hold values from -6 to 6
- lengths: int32 [32], P(('dp', 'neg')), may hold values from 256 to 512
- residual: bfloat16 [16384, 1024], P(('dp', 'neg')), may hold values from -6 to 6
- context: bfloat16 [16384, 1024], P(('dp', 'neg')), may hold values from -6 to 6
- out_proj: bfloat16 [1024, 1024], replicated, may hold values from -0.1875 to 0.1875
- norm_gain: float32 [1024], replicated, may hold values from 0.5 to 1.5
- colbert_proj: bfloat16 [1024, 128], replicated, may hold values from -0.1875 to 0.1875
Outputs:
- loss: float32 [], replicated
- query_grad: float32 [128, 32, 128], P(('dp', 'neg'))
- residual_grad: bfloat16 [16384, 1024], P(('dp', 'neg'))
- context_grad: bfloat16 [16384, 1024], P(('dp', 'neg'))
- out_proj_grad: float32 [1024, 1024], replicated
- colbert_grad: float32 [1024, 128], replicated
- gain_grad: float32 [1024], replicated
Inputs may be any that keep to these rules, and one draw needn't show every extreme that they name: A passage's first lengths[p] token slots are real, the rest padding.
All inputs are finite; a program needn't handle non-finite values.
Results may differ from a plain program's by a relative error of at most 0.0065.
Values may be sent and summed in bfloat16 or wider, within the bound.
A program may use at most 64 MiB of HBM per device.

v0:
```python
import math
import jax
import jax.numpy as jnp
from jax import lax
from jax.sharding import PartitionSpec as P


def combined_all(array, axis, combine):
    everything = jax.tree.map(lambda part: lax.all_gather(part, axis), array)
    initial = jax.tree.map(lambda part: part[0], everything)

    def turn(k, so_far):
        return combine(so_far, jax.tree.map(lambda part: part[k], everything))

    return lax.fori_loop(1, lax.axis_size(axis), turn, initial)


def block_plan(query_count, query_len):
    return math.gcd(query_count, max(1, 2048 // query_len))


def masked_scores(query_block, passage_one, usable):
    scores = jnp.einsum("rd,jd->rj", query_block, passage_one, preferred_element_type=jnp.float32)
    return jnp.where(usable, scores, -1e30)


def tile_forward(query_tokens, query_pos, passage_tokens, passage_len, passage_ids):
    query_count, query_len, emb_width = query_tokens.shape
    per_block = block_plan(query_count, query_len)
    query_blocks = query_tokens.reshape(query_count // per_block, per_block * query_len, emb_width)

    def per_passage(inputs):
        passage_one, length = inputs
        usable = (jnp.arange(passage_one.shape[0]) < length)[None, :]

        def per_query(query_block):
            masked = masked_scores(query_block, passage_one, usable)
            highest = jnp.max(masked, axis=1, keepdims=True)
            return highest[:, 0] + jnp.log(jnp.sum(jnp.exp(masked - highest), axis=1))

        inner_lse = lax.map(per_query, query_blocks).reshape(query_count, query_len)
        shifted = inner_lse - jnp.log(length.astype(jnp.float32))
        return (inner_lse, jnp.sum(shifted, axis=1))

    inner_all, similar = lax.map(per_passage, (passage_tokens, passage_len))
    similar = similar.T
    is_positive = passage_ids[None, :] == query_pos[:, None]
    highest = jnp.max(similar, axis=1)
    exp_total = jnp.sum(jnp.exp(similar - highest[:, None]), axis=1)
    positive_score = jnp.sum(jnp.where(is_positive, similar, 0.0), axis=1)
    return (inner_all, similar, is_positive, (highest, exp_total, positive_score))


def combine_totals(earlier, later):
    highest = jnp.maximum(earlier[0], later[0])
    exp_total = earlier[1] * jnp.exp(earlier[0] - highest) + later[1] * jnp.exp(later[0] - highest)
    return (highest, exp_total, earlier[2] + later[2])


def finish_rows(similar, is_positive, totals, own_block, query_dev):
    log_total = totals[0] + jnp.log(totals[1])
    coefficient = jnp.exp(similar - log_total[:, None]) - is_positive.astype(jnp.float32)
    own_terms = lax.dynamic_slice_in_dim(log_total - totals[2], own_block * query_dev, query_dev)
    return (coefficient, jnp.sum(own_terms))


def tile_backward(query_tokens, passage_tokens, passage_len, inner_all, coefficient):
    query_count, query_len, emb_width = query_tokens.shape
    per_block = block_plan(query_count, query_len)
    block_count = query_count // per_block
    query_blocks = query_tokens.reshape(block_count, per_block * query_len, emb_width)

    def per_passage(running, inputs):
        passage_one, length, inner_lse, column = inputs
        usable = (jnp.arange(passage_one.shape[0]) < length)[None, :]

        def per_query(pieces):
            query_block, inner_block, column_block = pieces
            masked = masked_scores(query_block, passage_one, usable)
            spread = jnp.exp(masked - inner_block.reshape(-1)[:, None]).reshape(
                per_block, query_len, -1
            )
            weight = (
                (spread * column_block[:, None, None])
                .reshape(per_block * query_len, -1)
                .astype(jnp.bfloat16)
            )
            query_part = jnp.dot(weight, passage_one, preferred_element_type=jnp.float32)
            passage_part = jnp.einsum(
                "rj,rd->jd", weight, query_block, preferred_element_type=jnp.float32
            )
            return (query_part, passage_part)

        query_parts, passage_parts = lax.map(
            per_query,
            (
                query_blocks,
                inner_lse.reshape(block_count, per_block, query_len),
                column.reshape(block_count, per_block),
            ),
        )
        return (running + query_parts.reshape(running.shape), jnp.sum(passage_parts, axis=0))

    start = jnp.zeros((query_count * query_len, emb_width), jnp.float32)
    query_sum, passage_sum = lax.scan(
        per_passage, start, (passage_tokens, passage_len, inner_all, coefficient.T)
    )
    return (query_sum.reshape(query_count, query_len, emb_width), passage_sum)


def window_rows(resid_rows, context_rows, grad_rows, out_proj, norm_gain, colbert_proj):
    hidden = resid_rows.astype(jnp.float32) + jnp.dot(
        context_rows, out_proj, preferred_element_type=jnp.float32
    )
    row_mean = jnp.mean(hidden, axis=1, keepdims=True)
    centred = hidden - row_mean
    variance = jnp.mean(centred * centred, axis=1, keepdims=True)
    inv_std = 1.0 / jnp.sqrt(variance + 1e-05)
    normed = centred * inv_std
    scaled = (normed * norm_gain).astype(jnp.bfloat16)
    colbert_part = jnp.dot(scaled.T, grad_rows, preferred_element_type=jnp.float32)
    scaled_grad = jnp.dot(grad_rows, colbert_proj.T, preferred_element_type=jnp.float32)
    gain_part = jnp.sum(scaled_grad * normed, axis=0)
    gained = scaled_grad * norm_gain
    hidden_grad = (
        inv_std
        * (
            gained
            - jnp.mean(gained, axis=1, keepdims=True)
            - normed * jnp.mean(gained * normed, axis=1, keepdims=True)
        )
    ).astype(jnp.bfloat16)
    context_grad = jnp.dot(hidden_grad, out_proj.T, preferred_element_type=jnp.float32).astype(
        jnp.bfloat16
    )
    proj_part = jnp.dot(context_rows.T, hidden_grad, preferred_element_type=jnp.float32)
    return (hidden_grad, context_grad, proj_part, colbert_part, gain_part)


def body(
    query_emb, positive, passage_emb, lengths, residual, context, out_proj, norm_gain, colbert_proj
):
    query_dev = query_emb.shape[0]
    passage_dev = passage_emb.shape[0]
    neg_size = lax.axis_size("neg")
    neg_place = lax.axis_index("neg")
    query_tokens, query_pos = (
        lax.all_gather(query_emb, "neg", axis=0, tiled=True),
        lax.all_gather(positive, "neg", axis=0, tiled=True),
    )
    passage_tokens, passage_len = (
        lax.all_gather(passage_emb, "dp", axis=0, tiled=True),
        lax.all_gather(lengths, "dp", axis=0, tiled=True),
    )
    position = jnp.arange(passage_tokens.shape[0], dtype=jnp.int32)
    passage_ids = (
        position // passage_dev * neg_size + neg_place
    ) * passage_dev + position % passage_dev
    inner_all, similar, is_positive, stats = tile_forward(
        query_tokens, query_pos, passage_tokens, passage_len, passage_ids
    )
    totals = combined_all(stats, "neg", combine_totals)
    coefficient, loss_part = finish_rows(similar, is_positive, totals, neg_place, query_dev)
    query_sum, passage_sum = tile_backward(
        query_tokens, passage_tokens, passage_len, inner_all, coefficient
    )
    query_grad = lax.psum_scatter(query_sum, "neg", scatter_dimension=0, tiled=True)
    emb_sum = lax.psum_scatter(passage_sum, "dp", scatter_dimension=0, tiled=True)
    emb_grad = emb_sum.astype(jnp.bfloat16).reshape(
        passage_dev * emb_sum.shape[1], emb_sum.shape[2]
    )
    residual_grad, context_grad, proj_part, colbert_part, gain_part = window_rows(
        residual, context, emb_grad, out_proj, norm_gain, colbert_proj
    )
    out_proj_grad, colbert_grad, gain_grad, loss_total = lax.psum(
        (proj_part, colbert_part, gain_part, loss_part), ("dp", "neg")
    )
    loss = loss_total / (query_dev * lax.axis_size("dp") * neg_size)
    return (loss, query_grad, residual_grad, context_grad, out_proj_grad, colbert_grad, gain_grad)


def solution(mesh):
    in_specs = (
        P(("dp", "neg"), None, None),
        P(("dp", "neg")),
        P(("dp", "neg"), None, None),
        P(("dp", "neg")),
        P(("dp", "neg"), None),
        P(("dp", "neg"), None),
        P(),
        P(),
        P(),
    )
    out_specs = (
        P(),
        P(("dp", "neg"), None, None),
        P(("dp", "neg"), None),
        P(("dp", "neg"), None),
        P(),
        P(),
        P(),
    )
    return jax.shard_map(body, mesh=mesh, in_specs=in_specs, out_specs=out_specs, check_vma=False)
```

profile of v0, /device:TPU:0, one launch (start us, length us, event | category | flops | bytes accessed | tf_op | source)
XLA Modules:
  0.0 304.9 jit_solution(8071022490365719969)
XLA Ops:
  8.9 1.2 dynamic-slice
  10.1 0.8 dynamic-update-slice
  10.9 9.9 %all-reduce = s32[4]{0:T(128)S(1)} all-reduce(s32[4]{0:T(128)S(1)} %dynamic-update-slice), channel_id=1, replica_groups=mesh['dp'=4,'neg'=8] {'dp'}, use_global_device_ids=true, to_apply=%add | all-reduce | flops 4 | bytes 32
  20.8 16.9 %all_gather.31 = bf16[4,512,128]{2,1,0:T(8,128)(2,1)} all-gather(bf16[1,512,128]{2,1,0:T(8,128)(2,1)} %param.17), channel_id=1, replica_groups=mesh['dp'=4,'neg'=8] {'dp'}, dimensions={0}, use_global_device_ids=true | all-gather | bytes 655360 | tf_op jit(solution)/shard_map/all_gather | solution.py:152
  37.7 9.5 %all_gather.32 = bf16[32,32,128]{2,1,0:T(8,128)(2,1)S(1)} all-gather(bf16[4,32,128]{2,1,0:T(8,128)(2,1)} %param.15), channel_id=1, replica_groups=mesh['dp'=4,'neg'=8] {'neg'}, dimensions={0}, use_global_device_ids=true | all-gather | bytes 294912 | tf_op jit(solution)/shard_map/all_gather | solution.py:148
  47.2 16.2 %while.53 = (s32[]{:T(128)}, f32[4,32,32]{2,1,0:T(8,128)S(1)}, f32[4,32]{1,0:T(4,128)S(1)}, s32[4]{0:T(128)S(1)}, bf16[4,512,128]{2,1,0:T(8,128)(2,1)}, /*index=...) while((s32[]{:T(128)}, f32[4,32,32]{2,1,0:T(8,128)S(1)}, f32[4,32]{1,0:T(4,128)S(1)}, ...), condition=%wide.region_4.5_spmd, body=%wide.region_0.4_spmd.sunk | while | flops 136840672 | bytes 4672013 | solution.py:45
  47.8 0.6 iota_compare_fusion.4
  48.4 1.4 select_reduce_fusion.2
  51.8 0.6 iota_compare_fusion.4
  52.5 1.4 select_reduce_fusion.2
  55.9 0.6 iota_compare_fusion.4
  56.5 1.4 select_reduce_fusion.2
  59.9 0.6 iota_compare_fusion.4
  60.6 1.4 select_reduce_fusion.2
  64.9 7.1 %all-reduce.3 = s32[32]{0:T(128)S(1)} all-reduce(s32[32]{0:T(128)S(1)} %dynamic-update-slice.3), channel_id=1, replica_groups=mesh['dp'=4,'neg'=8] {'neg'}, use_global_device_ids=true, to_apply=%add.3 | all-reduce | flops 32 | bytes 256
  73.4 11.8 %all-reduce.7 = (f32[256]{0:T(256)S(1)}, f32[256]{0:T(256)S(1)}, f32[256]{0:T(256)S(1)}) all-reduce(f32[256]{0:T(256)S(1)} %dynamic-update-slice.1, f32[256]{0:T(256)S(1)} %dynamic-update-slice.2, f32[256]{0:T(256)S(1)} %dynamic-update-slice.4), channel_id=2, replica_groups=mesh['dp'=4,'neg'=8] {'neg'}, use_global_device_ids=true, to_apply=%add.1 | all-reduce | flops 768 | bytes 6144
  85.8 25.8 %while.55 = (s32[]{:T(128)}, f32[1024,128]{1,0:T(8,128)}, f32[4,512,128]{2,1,0:T(8,128)}, s32[4]{0:T(128)S(1)}, bf16[4,512,128]{2,1,0:T(8,128)(2,1)}, /*index=5*...) while((s32[]{:T(128)}, f32[1024,128]{1,0:T(8,128)}, ...), condition=%wide.region_13.14_spmd.clone, body=%wide.region_12.13_spmd.clone.sunk | while | flops 405012992 | bytes 5282823 | solution.py:105
  86.1 0.6 dynamic_slice.125
  86.7 0.6 iota_compare_fusion.5
  87.3 1.5 multiply_convert_fusion.5
  88.8 1.2 fusion.63
  90.0 2.2 convolution_add_fusion.2
  93.0 0.6 iota_compare_fusion.5
  93.6 1.5 multiply_convert_fusion.5
  95.1 1.1 fusion.63
  96.2 2.4 convolution_add_fusion.2
  99.4 0.6 iota_compare_fusion.5
  100.1 1.5 multiply_convert_fusion.5
  101.6 1.1 fusion.63
  102.7 2.4 convolution_add_fusion.2
  105.9 0.6 iota_compare_fusion.5
  106.6 1.5 multiply_convert_fusion.5
  108.1 1.1 fusion.63
  109.2 2.4 convolution_add_fusion.2
  111.7 2.9 fusion.36
  114.6 1.3 copy-done.1
  116.2 21.0 %reduce-scatter.5.cloned.1.call-done = f32[1,512,128]{2,1,0:T(8,128)} async-done(((f32[4,512,128]{2,1,0:T(8,128)}), f32[1,512,128]{2,1,0:T(8,128)}) %reduce-scatter.5.cloned.1.call-update) | async-done | bytes 262160 | tf_op jit(solution)/shard_map/reduce_scatter | solution.py:168
  137.3 2.7 multiply_reduce_fusion
  140.0 0.6 multiply_convert_fusion.2
  140.6 0.6 copy-done.5
  141.2 3.3 %convolution_bitcast_fusion.1 = f32[1024,1024]{0,1:T(8,128)} fusion(bf16[512,1024]{1,0:T(8,128)(2,1)S(1)} %multiply_convert_fusion.2, bf16[512,1024]{1,0:T(8,128)(2,1)S(1)} %copy-done.5), kind=kOutput, calls=%fused_computation.37 | convolution fusion | flops 1073741824 | bytes 6291456 | tf_op jit(solution)/shard_map/dot_general | solution.py:136
  144.5 1.6 fusion.22
  146.7 0.7 dynamic-slice_reduce_fusion
  147.4 39.7 %all-reduce.5 = (f32[]{:T(128)}, f32[1024]{0:T(1024)}) all-reduce(f32[]{:T(128)} %dynamic-slice_reduce_fusion, f32[1024]{0:T(1024)S(1)} %get-tuple-element.355), channel_id=1, replica_groups=mesh['dp'=4,'neg'=8] {'dp','neg'}, use_global_device_ids=true, to_apply=%region_11.12 | all-reduce | flops 1025 | bytes 8200 | tf_op jit(solution)/shard_map/psum | solution.py:175
  187.7 2.3 convolution_convert_fusion
  190.0 100.1 %all-reduce.10.cloned.1.call-done = (f32[1024,1024]{0,1:T(8,128)}, f32[1024,128]{1,0:T(8,128)}) async-done(((f32[1024,1024]{0,1:T(8,128)}, f32[1024,128]{1,0:T(8,128)}), (f32[1024,1024]{0,1:T(8,128)}, f32[1024,128]{1,0:T(8,128)})) %all-reduce.10.cloned.1.call-update) | async-done | bytes 4718608 | tf_op jit(solution)/shard_map/psum | solution.py:175
  290.1 5.4 %copy.18 = f32[1024,1024]{1,0:T(8,128)} copy(f32[1024,1024]{0,1:T(8,128)} %get-tuple-element.404) | data formatting | bytes 8388608
  295.5 0.8 copy.61
  (119 shorter events, 11.5 us)
Async XLA Ops:
  8.0 103.7 %copy-start = (bf16[1024,1024]{1,0:T(8,128)(2,1)S(1)}, bf16[1024,1024]{1,0:T(8,128)(2,1)}, u32[]{:S(2)}) copy-start(bf16[1024,1024]{1,0:T(8,128)(2,1)} %param.21) | copy-start | bytes 6291460
  8.0 129.2 %reduce-scatter.5.cloned.1.call-start = ((), (), s32[]{:S(2)}) async-start(), calls=%async_computation.3 | async-start | bytes 1310720 | tf_op jit(solution)/shard_map/reduce_scatter | solution.py:168
  47.2 16.2 %copy-start.10 = (u32[32]{0:T(128)S(1)}, u32[32]{0:T(128)}, u32[]{:S(2)}) copy-start(u32[32]{0:T(128)} %constant.164) | copy-start | bytes 388
  47.2 17.5 %copy-start.9 = (s32[4]{0:T(128)S(1)}, s32[4]{0:T(128)}, u32[]{:S(2)}) copy-start(s32[4]{0:T(128)} %param.16) | copy-start | bytes 52
  111.6 178.5 %all-reduce.10.cloned.1.call-start = ((), (), s32[]{:S(2)}) async-start(), calls=%async_computation.4 | async-start | bytes 9437184 | tf_op jit(solution)/shard_map/psum | solution.py:175
  114.6 1.3 copy-start.1
  114.6 22.7 %copy-start.7 = (bf16[1024,128]{1,0:T(8,128)(2,1)S(1)}, bf16[1024,128]{1,0:T(8,128)(2,1)}, u32[]{:S(2)}) copy-start(bf16[1024,128]{1,0:T(8,128)(2,1)} %param.23) | copy-start | bytes 786436
  114.6 22.7 %copy-start.8 = (f32[1024]{0:T(1024)S(1)}, f32[1024]{0:T(1024)}, u32[]{:S(2)}) copy-start(f32[1024]{0:T(1024)} %param.22) | copy-start | bytes 12292
  137.3 2.7 copy-start.2
  140.0 1.2 copy-start.5
  141.2 46.5 %copy-start.3 = (bf16[512,1024]{1,0:T(8,128)(2,1)}, bf16[512,1024]{1,0:T(8,128)(2,1)S(1)}, u32[]{:S(2)}) copy-start(bf16[512,1024]{1,0:T(8,128)(2,1)S(1)} %multiply_convert_fusion.2) | copy-start | bytes 3145732
  141.2 3.3 %copy-start.4 = (f32[1,512,128]{2,1,0:T(8,128)S(1)}, f32[1,512,128]{2,1,0:T(8,128)}, u32[]{:S(2)}) copy-start(f32[1,512,128]{2,1,0:T(8,128)} %reduce-scatter.5.cloned.1.call-done) | copy-start | bytes 786436
  146.1 149.4 %reduce-scatter.3.cloned.1.call-start = ((), (), s32[]{:S(2)}) async-start(), calls=%async_computation.2 | async-start | bytes 589824 | tf_op jit(solution)/shard_map/reduce_scatter | solution.py:167
  290.1 5.4 %copy-start.6 = (f32[1024,128]{1,0:T(8,128)S(1)}, f32[1024,128]{1,0:T(8,128)}, u32[]{:S(2)}) copy-start(f32[1024,128]{1,0:T(8,128)} %get-tuple-element.658) | copy-start | bytes 1572868
Sparse Core Ops, SparseCore 0:
  111.7 25.4 reduce-scatter.4
  146.3 143.7 all-reduce.9
Sparse Core Ops, SparseCore 1:
  150.3 32.6 reduce-scatter.2
where the time goes:
time: 306 us; the launch traced here: 305 us
  waiting for transfers between devices  122 us (40%)
  blocking collectives  94.9 us (31%)
  matrix products  38 us (12%)
  between operations  19.5 us (6%)
  local copies, waits for them, and re-layouts  18.2 us (6%)
  other arithmetic  9.43 us (3%)
  loops' own time  3.07 us (1%)
    psum x1, waiting for transfers between devices, body(): lax.psum((proj_part, colbert_part, gain_part, loss_part), ('dp', 'neg'))  100 us
    psum x1, blocking collectives, body(): lax.psum((proj_part, colbert_part, gain_part, loss_part), ('dp', 'neg'))  39.7 us
    unnamed x3, blocking collectives  28.8 us
    reduce_scatter x1, waiting for transfers between devices, body(): lax.psum_scatter(passage_sum, 'dp', scatter_dimension=0, tiled=True)  21 us
    all_gather x1, blocking collectives, body(): lax.all_gather(passage_emb, 'dp', axis=0, tiled=True)  16.9 us
    unnamed x36, local copies, waits for them, and re-layouts  11.6 us
    dot_general x8, matrix products, masked_scores(): jnp.einsum('rd,jd->rj', query_block, passage_one, preferred_element_type=...  11.4 us
    all_gather x1, blocking collectives, body(): lax.all_gather(query_emb, 'neg', axis=0, tiled=True)  9.51 us
  transfers between devices with their start and end apart: 3, of which 2 were waited for; matrix products, arithmetic and copies ran while one was open for 4% of the time, Pallas kernels for 0%

commit v1 on v0

--- a/solution.py
+++ b/solution.py
@@ -3,6 +3,13 @@
 import jax.numpy as jnp
 from jax import lax
 from jax.sharding import PartitionSpec as P
+from jax.lax import psum
+
+
+def draw_the_signs(arr, across, mesh_dim):
+    for idx in (across, mesh_dim):
+        arr = psum(arr, idx)
+    return arr
 
 
 def combined_all(array, axis, combine):
@@ -172,8 +179,8 @@
     residual_grad, context_grad, proj_part, colbert_part, gain_part = window_rows(
         residual, context, emb_grad, out_proj, norm_gain, colbert_proj
     )
-    out_proj_grad, colbert_grad, gain_grad, loss_total = lax.psum(
-        (proj_part, colbert_part, gain_part, loss_part), ("dp", "neg")
+    out_proj_grad, colbert_grad, gain_grad, loss_total = draw_the_signs(
+        (proj_part, colbert_part, gain_part, loss_part), "dp", "neg"
     )
     loss = loss_total / (query_dev * lax.axis_size("dp") * neg_size)
     return (loss, query_grad, residual_grad, context_grad, out_proj_grad, colbert_grad, gain_grad)

time: 306 us -> 453 us (1.48)
  waiting for transfers between devices: 122 us -> 286 us
  blocking collectives: 94.9 us -> 79.5 us
    psum x1 -> x2, waiting for transfers between devices: 100 us -> 232 us  [draw_the_signs(): arr = psum(arr, idx)]
    reduce_scatter x1, waiting for transfers between devices: 0.01 us -> 32.3 us  [body(): lax.psum_scatter(query_sum, 'neg', scatter_dimension=0, tiled=True)]
    psum x1 -> x2, blocking collectives: 39.7 us -> 24.3 us  [draw_the_signs(): arr = psum(arr, idx)]
  transfers between devices with their start and end apart: 3 -> 4, of which waited for: 2 -> 4; matrix products, arithmetic and copies ran while one was open for 4% -> 3% of each run, Pallas kernels for 0% -> 0%
where the time goes in v1:
time: 453 us; the launch traced here: 452 us
  waiting for transfers between devices  286 us (63%)
  blocking collectives  79.5 us (18%)
  matrix products  38 us (8%)
  local copies, waits for them, and re-layouts  18.2 us (4%)
  between operations  17.8 us (4%)
  other arithmetic  9.43 us (2%)
    psum x2, waiting for transfers between devices, draw_the_signs(): arr = psum(arr, idx)  232 us
    reduce_scatter x1, waiting for transfers between devices, body(): lax.psum_scatter(query_sum, 'neg', scatter_dimension=0, tiled=True)  32.3 us
    unnamed x3, blocking collectives  28.8 us
    psum x2, blocking collectives, draw_the_signs(): arr = psum(arr, idx)  24.3 us
    reduce_scatter x1, waiting for transfers between devices, body(): lax.psum_scatter(passage_sum, 'dp', scatter_dimension=0, tiled=True)  21 us
    all_gather x1, blocking collectives, body(): lax.all_gather(passage_emb, 'dp', axis=0, tiled=True)  16.9 us
    unnamed x36, local copies, waits for them, and re-layouts  11.6 us
    dot_general x8, matrix products, masked_scores(): jnp.einsum('rd,jd->rj', query_block, passage_one, preferred_element_type=...  11.3 us
  transfers between devices with their start and end apart: 4, of which 4 were waited for; matrix products, arithmetic and copies ran while one was open for 3% of the time, Pallas kernels for 0%

profile of v1, /device:TPU:0, one launch (start us, length us, event | category | flops | bytes accessed | tf_op | source)
XLA Modules:
  0.0 451.7 jit_solution(12295078461135185338)
XLA Ops:
  8.0 1.2 dynamic-slice
  9.3 0.8 dynamic-update-slice
  10.0 9.9 %all-reduce = s32[4]{0:T(128)S(1)} all-reduce(s32[4]{0:T(128)S(1)} %dynamic-update-slice), channel_id=1, replica_groups=mesh['dp'=4,'neg'=8] {'dp'}, use_global_device_ids=true, to_apply=%add | all-reduce | flops 4 | bytes 32
  20.0 16.9 %all_gather.31 = bf16[4,512,128]{2,1,0:T(8,128)(2,1)} all-gather(bf16[1,512,128]{2,1,0:T(8,128)(2,1)} %param.17), channel_id=1, replica_groups=mesh['dp'=4,'neg'=8] {'dp'}, dimensions={0}, use_global_device_ids=true | all-gather | bytes 655360 | tf_op jit(solution)/shard_map/all_gather | solution.py:159
  36.8 9.5 %all_gather.32 = bf16[32,32,128]{2,1,0:T(8,128)(2,1)S(1)} all-gather(bf16[4,32,128]{2,1,0:T(8,128)(2,1)} %param.15), channel_id=1, replica_groups=mesh['dp'=4,'neg'=8] {'neg'}, dimensions={0}, use_global_device_ids=true | all-gather | bytes 294912 | tf_op jit(solution)/shard_map/all_gather | solution.py:155
  46.3 16.2 %while.53 = (s32[]{:T(128)}, f32[4,32,32]{2,1,0:T(8,128)S(1)}, f32[4,32]{1,0:T(4,128)S(1)}, s32[4]{0:T(128)S(1)}, bf16[4,512,128]{2,1,0:T(8,128)(2,1)}, /*index=...) while((s32[]{:T(128)}, f32[4,32,32]{2,1,0:T(8,128)S(1)}, f32[4,32]{1,0:T(4,128)S(1)}, ...), condition=%wide.region_4.5_spmd, body=%wide.region_0.4_spmd.sunk | while | flops 136840672 | bytes 4672013 | solution.py:52
  46.9 0.6 iota_compare_fusion.4
  47.6 1.4 select_reduce_fusion.2
  51.0 0.6 iota_compare_fusion.4
  51.6 1.4 select_reduce_fusion.2
  55.0 0.6 iota_compare_fusion.4
  55.7 1.4 select_reduce_fusion.2
  59.1 0.6 iota_compare_fusion.4
  59.7 1.4 select_reduce_fusion.2
  64.1 7.1 %all-reduce.3 = s32[32]{0:T(128)S(1)} all-reduce(s32[32]{0:T(128)S(1)} %dynamic-update-slice.3), channel_id=1, replica_groups=mesh['dp'=4,'neg'=8] {'neg'}, use_global_device_ids=true, to_apply=%add.3 | all-reduce | flops 32 | bytes 256
  72.6 11.8 %all-reduce.6 = (f32[256]{0:T(256)S(1)}, f32[256]{0:T(256)S(1)}, f32[256]{0:T(256)S(1)}) all-reduce(f32[256]{0:T(256)S(1)} %dynamic-update-slice.1, f32[256]{0:T(256)S(1)} %dynamic-update-slice.2, f32[256]{0:T(256)S(1)} %dynamic-update-slice.4), channel_id=2, replica_groups=mesh['dp'=4,'neg'=8] {'neg'}, use_global_device_ids=true, to_apply=%add.1 | all-reduce | flops 768 | bytes 6144
  85.0 25.8 %while.55 = (s32[]{:T(128)}, f32[1024,128]{1,0:T(8,128)}, f32[4,512,128]{2,1,0:T(8,128)}, s32[4]{0:T(128)S(1)}, bf16[4,512,128]{2,1,0:T(8,128)(2,1)}, /*index=5*...) while((s32[]{:T(128)}, f32[1024,128]{1,0:T(8,128)}, ...), condition=%wide.region_14.15_spmd.clone, body=%wide.region_13.14_spmd.clone.sunk | while | flops 405012992 | bytes 5282823 | solution.py:112
  85.8 0.6 iota_compare_fusion.5
  86.5 1.5 multiply_convert_fusion.5
  88.0 1.2 fusion.63
  89.1 2.2 convolution_add_fusion.2
  92.1 0.6 iota_compare_fusion.5
  92.8 1.5 multiply_convert_fusion.5
  94.3 1.1 fusion.63
  95.4 2.4 convolution_add_fusion.2
  98.6 0.6 iota_compare_fusion.5
  99.3 1.5 multiply_convert_fusion.5
  100.7 1.1 fusion.63
  101.9 2.4 convolution_add_fusion.2
  105.1 0.6 iota_compare_fusion.5
  105.7 1.5 multiply_convert_fusion.5
  107.2 1.1 fusion.63
  108.4 2.4 convolution_add_fusion.2
  110.8 2.9 fusion.36
  113.8 1.3 copy-done.1
  115.4 21.0 %reduce-scatter.5.cloned.1.call-done = f32[1,512,128]{2,1,0:T(8,128)} async-done(((f32[4,512,128]{2,1,0:T(8,128)}), f32[1,512,128]{2,1,0:T(8,128)}) %reduce-scatter.5.cloned.1.call-update) | async-done | bytes 262160 | tf_op jit(solution)/shard_map/reduce_scatter | solution.py:175
  136.4 2.7 multiply_reduce_fusion
  140.4 3.3 convolution_bitcast_fusion.1
  143.7 1.6 fusion.22
  145.4 170.6 %all-reduce.15.cloned.1.call-done = (f32[1024,1024]{0,1:T(8,128)}, f32[1024,128]{1,0:T(8,128)}) async-done(((f32[1024,1024]{0,1:T(8,128)}, f32[1024,128]{1,0:T(8,128)}), (f32[1024,1024]{0,1:T(8,128)}, f32[1024,128]{1,0:T(8,128)})) %all-reduce.15.cloned.1.call-update) | async-done | bytes 4718608 | tf_op jit(solution)/shard_map/psum | solution.py:11
  316.5 0.7 dynamic-slice_reduce_fusion
  317.2 10.2 %all-reduce.8 = (f32[]{:T(128)}, f32[1024]{0:T(1024)S(1)}) all-reduce(f32[]{:T(128)} %dynamic-slice_reduce_fusion, f32[1024]{0:T(1024)S(1)} %get-tuple-element.355), channel_id=1, replica_groups=mesh['dp'=4,'neg'=8] {'dp'}, use_global_device_ids=true, to_apply=%region_11.12 | all-reduce | flops 1025 | bytes 8200 | tf_op jit(solution)/shard_map/psum | solution.py:11
  327.4 14.2 %all-reduce.5 = (f32[]{:T(128)}, f32[1024]{0:T(1024)}) all-reduce(f32[]{:T(128)} %get-tuple-element.409, f32[1024]{0:T(1024)S(1)} %get-tuple-element.410), channel_id=1, replica_groups=mesh['dp'=4,'neg'=8] {'neg'}, use_global_device_ids=true, to_apply=%region_12.13 | all-reduce | flops 1025 | bytes 8200 | tf_op jit(solution)/shard_map/psum | solution.py:11
  342.2 2.3 convolution_convert_fusion
  344.4 61.1 %all-reduce.13.cloned.1.call-done = (f32[1024,1024]{0,1:T(8,128)}, f32[1024,128]{1,0:T(8,128)}) async-done(((f32[1024,1024]{0,1:T(8,128)}, f32[1024,128]{1,0:T(8,128)}), (f32[1024,1024]{0,1:T(8,128)}, f32[1024,128]{1,0:T(8,128)})) %all-reduce.13.cloned.1.call-update) | async-done | bytes 4718608 | tf_op jit(solution)/shard_map/psum | solution.py:11
  405.5 5.4 %copy.18 = f32[1024,1024]{1,0:T(8,128)} copy(f32[1024,1024]{0,1:T(8,128)} %get-tuple-element.407) | data formatting | bytes 8388608
  410.9 32.3 %reduce-scatter.3.cloned.1.call-done = f32[4,32,128]{2,1,0:T(8,128)} async-done(((f32[32,32,128]{2,1,0:T(8,128)}), f32[4,32,128]{2,1,0:T(8,128)}) %reduce-scatter.3.cloned.1.call-update) | async-done | bytes 65552 | tf_op jit(solution)/shard_map/reduce_scatter | solution.py:174
  443.3 0.8 copy.63
  (123 shorter events, 13.3 us)
Async XLA Ops:
  7.2 103.7 %copy-start = (bf16[1024,1024]{1,0:T(8,128)(2,1)S(1)}, bf16[1024,1024]{1,0:T(8,128)(2,1)}, u32[]{:S(2)}) copy-start(bf16[1024,1024]{1,0:T(8,128)(2,1)} %param.21) | copy-start | bytes 6291460
  7.2 129.3 %reduce-scatter.5.cloned.1.call-start = ((), (), s32[]{:S(2)}) async-start(), calls=%async_computation.3 | async-start | bytes 1310720 | tf_op jit(solution)/shard_map/reduce_scatter | solution.py:175
  46.3 16.2 %copy-start.10 = (u32[32]{0:T(128)S(1)}, u32[32]{0:T(128)}, u32[]{:S(2)}) copy-start(u32[32]{0:T(128)} %constant.164) | copy-start | bytes 388
  46.3 17.5 %copy-start.9 = (s32[4]{0:T(128)S(1)}, s32[4]{0:T(128)}, u32[]{:S(2)}) copy-start(s32[4]{0:T(128)} %param.16) | copy-start | bytes 52
  110.8 205.1 %all-reduce.15.cloned.1.call-start = ((), (), s32[]{:S(2)}) async-start(), calls=%async_computation.5 | async-start | bytes 9437184 | tf_op jit(solution)/shard_map/psum | solution.py:11
  113.7 1.3 copy-start.1
  113.7 22.7 %copy-start.7 = (bf16[1024,128]{1,0:T(8,128)(2,1)S(1)}, bf16[1024,128]{1,0:T(8,128)(2,1)}, u32[]{:S(2)}) copy-start(bf16[1024,128]{1,0:T(8,128)(2,1)} %param.23) | copy-start | bytes 786436
  113.7 22.7 %copy-start.8 = (f32[1024]{0:T(1024)S(1)}, f32[1024]{0:T(1024)}, u32[]{:S(2)}) copy-start(f32[1024]{0:T(1024)} %param.22) | copy-start | bytes 12292
  136.4 2.7 copy-start.2
  139.2 1.2 copy-start.5
  140.4 201.8 %copy-start.3 = (bf16[512,1024]{1,0:T(8,128)(2,1)}, bf16[512,1024]{1,0:T(8,128)(2,1)S(1)}, u32[]{:S(2)}) copy-start(bf16[512,1024]{1,0:T(8,128)(2,1)S(1)} %multiply_convert_fusion.2) | copy-start | bytes 3145732
  140.4 3.3 copy-start.4
  145.3 260.2 %all-reduce.13.cloned.1.call-start = ((), (), s32[]{:S(2)}) async-start(), calls=%async_computation.4 | async-start | bytes 9437184 | tf_op jit(solution)/shard_map/psum | solution.py:11
  315.9 127.3 %reduce-scatter.3.cloned.1.call-start = ((), (), s32[]{:S(2)}) async-start(), calls=%async_computation.2 | async-start | bytes 589824 | tf_op jit(solution)/shard_map/reduce_scatter | solution.py:174
  405.5 37.7 %copy-start.6 = (f32[1024,128]{1,0:T(8,128)S(1)}, f32[1024,128]{1,0:T(8,128)}, u32[]{:S(2)}) copy-start(f32[1024,128]{1,0:T(8,128)} %get-tuple-element.662) | copy-start | bytes 1572868
Sparse Core Ops, SparseCore 0:
  110.9 25.4 reduce-scatter.4
  145.4 170.4 all-reduce.14
  319.3 86.1 all-reduce.12
  409.0 34.1 reduce-scatter.2
